TPU v7x, 32 devices: a whole 2x2x4 slice. The times are simulated.
32 devices in a mesh: src: 4 (over y, x), blk: 8 (over z, core).
Axes of the slice: x: 2, y: 2, z: 4, core: 2. Of those that a mesh axis runs over, the one named last changes fastest.
Arguments:
- values: float32 [4, 512, 32, 128], P('src', 'blk'), may hold values from -0.25 to 0.25
- diagonal: float32 [4, 512, 128], P('src', 'blk'), may hold values from 0.55 to 0.95
- rhs_parts: float32 [4, 512, 128], P('src', 'blk'), may hold values from -24 to 24
- owner_map: int32 [512, 128], P('blk'), may hold values from 0 to 3
- columns: int32 [512, 32, 128], P('blk'), may hold values from 0 to 1073741823
- destination: int32 [512, 1], P('blk'), may hold values from 0 to 7; in each aligned block of 64 rows (0 to 63, 64 to 127, ...) at most 16 rows name the same one
- order_keys: int32 [512], P('blk'), may hold values from 0 to 511, each once
Outputs:
- solution: float32 [512, 128], P('blk')
Inputs may be any that keep to these rules, and one draw needn't show every extreme that they name: `destination`: among the row blocks of one index of blk no owner is named more than 16 times, some owner is named exactly 16 times, and every owner is named by some block. `order_keys`: each key appears once.
All inputs are finite; a program needn't handle non-finite values.
Results may differ from a plain program's by a relative error of at most 0.0003.
Values sent between devices are 32-bit elements; how exact they have to be, the bound alone decides.
No kernel may reach another device: no remote copies, remote signals or barrier semaphores. Data moves between devices by JAX's collectives and lax.ppermute only.
A program may use at most 64 MiB of HBM per device.

v0:
```python
import jax
import jax.numpy as jnp
from jax import lax
from jax.sharding import PartitionSpec as P

SWEEPS = 3


def tile_matrix(block_vals, block_cols, tile_rows):
    slot_count = block_vals.shape[0]
    stored = block_vals.shape[1]
    groups = 8
    lanes = jnp.remainder(block_cols, 2 * tile_rows)
    targets = jnp.arange(2 * tile_rows, dtype=jnp.int32)
    grouped_vals = block_vals.reshape(groups, slot_count // groups, stored, tile_rows)
    grouped_lanes = lanes.reshape(groups, slot_count // groups, stored, tile_rows)

    def build(pair):
        group_vals, group_lanes = pair
        picked = jnp.where(group_lanes[..., None] == targets, group_vals[..., None], 0.0)
        return jnp.sum(picked, axis=1)

    dense = lax.map(build, (grouped_vals, grouped_lanes))
    return dense.reshape(slot_count, tile_rows, 2 * tile_rows)


def on_device(values, diagonal, rhs_parts, owner_map, columns, destination, order_keys):
    owners = lax.axis_size("blk")
    part_count = lax.axis_size("src")
    tile_count = destination.shape[0]
    stored = values.shape[2]
    tile_rows = values.shape[3]
    per_peer = 2 * tile_count // owners
    slot_count = owners * per_peer
    owner_of = destination[:, 0]
    tile_ids = jnp.arange(tile_count, dtype=jnp.int32)
    slot_ids = jnp.arange(slot_count, dtype=jnp.int32)
    earlier = (owner_of[None, :] == owner_of[:, None]) & (tile_ids[None, :] < tile_ids[:, None])
    position = jnp.sum(earlier, axis=1)
    slot_of = owner_of * per_peer + position
    slot_hits = slot_of[None, :] == slot_ids[:, None]
    filled = jnp.any(slot_hits, axis=1)
    source_tile = jnp.sum(jnp.where(slot_hits, tile_ids[None, :], 0), axis=1)
    is_owned = owner_map == lax.axis_index("src")
    own_rhs = jnp.where(is_owned, rhs_parts[0], 0.0)
    send_vals = jnp.where(filled[:, None, None], values[0][source_tile], 0.0)
    send_diag = jnp.where(filled[:, None], diagonal[0][source_tile], 0.0)
    send_rhs = jnp.where(filled[:, None], own_rhs[source_tile], 0.0)
    send_cols = columns[source_tile]
    send_keys = jnp.where(filled, order_keys[source_tile], -1)
    quarter = stored // part_count
    part_vals = lax.psum_scatter(send_vals, "src", scatter_dimension=1, tiled=True)
    sum_diag, sum_rhs = lax.psum((send_diag, send_rhs), "src")
    part_cols = lax.dynamic_slice_in_dim(send_cols, lax.axis_index("src") * quarter, quarter, 1)
    got_vals, got_diag, got_rhs = (
        lax.all_to_all(part_vals, "blk", split_axis=0, concat_axis=0, tiled=True),
        lax.all_to_all(sum_diag, "blk", split_axis=0, concat_axis=0, tiled=True),
        lax.all_to_all(sum_rhs, "blk", split_axis=0, concat_axis=0, tiled=True),
    )
    got_cols, got_keys = (
        lax.all_to_all(part_cols, "blk", split_axis=0, concat_axis=0, tiled=True),
        lax.all_to_all(send_keys, "blk", split_axis=0, concat_axis=0, tiled=True),
    )
    is_live = got_keys >= 0
    tile_total = jnp.sum(is_live)
    smaller = is_live[None, :] & (got_keys[None, :] < got_keys[:, None])
    tile_rank = jnp.sum(smaller, axis=1)
    rank_hits = is_live[None, :] & (tile_rank[None, :] == slot_ids[:, None])
    holder = jnp.sum(jnp.where(rank_hits, slot_ids[None, :], 0), axis=1)
    occupied = slot_ids < tile_total
    block_vals = jnp.where(occupied[:, None, None], got_vals[holder], 0.0)
    block_cols = got_cols[holder]
    right_side = jnp.where(occupied[:, None], got_rhs[holder], 0.0)
    block_diag = jnp.where(occupied[:, None], got_diag[holder], 1.0)
    dense = tile_matrix(block_vals, block_cols, tile_rows)
    following = jnp.remainder(slot_ids + 1, tile_total)
    iterate = jnp.zeros((slot_count, tile_rows), jnp.float32)
    for sweep_index in range(SWEEPS):
        nearby = jnp.concatenate([iterate, iterate[following]], axis=1)
        partial_sum = jnp.sum(dense * nearby[:, None, :], axis=2)
        summed = lax.psum(partial_sum, "src")
        iterate = jnp.where(occupied[:, None], (right_side - summed) / block_diag, 0.0)
    in_slots = jnp.where(is_live[:, None], iterate[tile_rank], 0.0)
    returned = lax.all_to_all(in_slots, "blk", split_axis=0, concat_axis=0, tiled=True)
    return returned[slot_of]


def solution(mesh):
    placed = (
        P("src", "blk", None, None),
        P("src", "blk", None),
        P("src", "blk", None),
        P("blk", None),
        P("blk", None, None),
        P("blk", None),
        P("blk"),
    )
    return jax.shard_map(
        on_device, mesh=mesh, in_specs=placed, out_specs=P("blk", None), check_vma=False
    )
```

profile of v0, /device:TPU:0, one launch (start us, length us, event | category | flops | bytes accessed | tf_op | source)
XLA Modules:
  0.0 320.4 jit_solution(3956767261336183481)
XLA Ops:
  9.2 1.6 broadcast_select_fusion
  10.8 1.6 gather_fusion
  13.1 6.4 %all-to-all-start = ((s32[8,16,1]{1,2,0:T(1,128)}), s32[8,16,1]{1,2,0:T(1,128)S(1)}, u32[]{:S(2)}, u32[]{:S(2)}) async-start(s32[8,16,1]{1,2,0:T(1,128)} %bitcast.3), calls=%async_computation | async-start | bytes 8192 | tf_op jit(solution)/shard_map/all_to_all | solution.py:62
  19.4 2.2 gather_fusion.3
  22.5 2.4 all-to-all-done
  24.9 3.5 %all-to-all-start.2 = ((s32[128,8,128]{2,1,0:T(8,128)}), s32[128,8,128]{2,1,0:T(8,128)S(1)}, u32[]{:S(2)}, u32[]{:S(2)}) async-start(s32[128,8,128]{2,1,0:T(8,128)} %constant_dynamic-slice_fusion), calls=%async_computation.2 | async-start | bytes 1048576 | tf_op jit(solution)/shard_map/all_to_all | solution.py:61
  34.5 9.2 %all-to-all-done.2 = s32[128,8,128]{2,1,0:T(8,128)S(1)} async-done(((s32[128,8,128]{2,1,0:T(8,128)}), s32[128,8,128]{2,1,0:T(8,128)S(1)}, u32[]{:S(2)}, u32[]{:S(2)}) %all-to-all-start.2) | async-done | bytes 524320 | tf_op jit(solution)/shard_map/all_to_all | solution.py:61
  43.7 5.2 %reduce-scatter.2.cloned.1.call-done = f32[128,8,128]{2,1,0:T(8,128)} async-done(((f32[128,32,128]{2,1,0:T(8,128)}), f32[128,8,128]{2,1,0:T(8,128)}) %reduce-scatter.2.cloned.1.call-update) | async-done | bytes 524304 | tf_op jit(solution)/shard_map/reduce_scatter | solution.py:52
  48.9 4.6 %all-to-all-start.3 = ((f32[128,8,128]{2,1,0:T(8,128)}), f32[128,8,128]{2,1,0:T(8,128)S(1)}, u32[]{:S(2)}, u32[]{:S(2)}) async-start(f32[128,8,128]{2,1,0:T(8,128)} %reduce-scatter.2.cloned.1.call-done), calls=%async_computation.4 | async-start | bytes 1048576 | tf_op jit(solution)/shard_map/all_to_all | solution.py:56
  55.5 13.3 %all-to-all-done.3 = f32[128,8,128]{2,1,0:T(8,128)S(1)} async-done(((f32[128,8,128]{2,1,0:T(8,128)}), f32[128,8,128]{2,1,0:T(8,128)S(1)}, u32[]{:S(2)}, u32[]{:S(2)}) %all-to-all-start.3) | async-done | bytes 524320 | tf_op jit(solution)/shard_map/all_to_all | solution.py:56
  69.8 57.8 %while.11 = (s32[]{:T(128)}, f32[8,16,128,256]{3,2,1,0:T(8,128)}, s32[8,16,8,128]{3,2,1,0:T(8,128)S(1)}, f32[8,16,8,128]{3,2,1,0:T(8,128)S(1)}, s32[]{:T(128)}) while((s32[]{:T(128)}, f32[8,16,128,256]{3,2,1,0:T(8,128)}, s32[8,16,8,128]{3,2,1,0:T(8,128)S(1)}, f32[8,16,8,128]{3,2,1,0:T(8,128)S(1)}, s32[]{:T(128)}) %tuple.23), condition=%wide.region_10.11_spmd.clone, body=%wide.region_8.10_spmd.clone.sunk | while | flops 12058626 | bytes 6685253 | solution.py:23
  69.8 5.7 %select_reduce_fusion.4 = f32[16,128,256]{2,1,0:T(8,128)S(1)} fusion(f32[16,8,128]{2,1,0:T(8,128)S(1)} %dynamic-slice_bitcast_fusion.4, s32[16,8,128]{2,1,0:T(8,128)S(1)} %dynamic-slice_bitcast_fusion.5), kind=kLoop, calls=%fused_computation.16.clone.1 | loop fusion | flops 12058624 | bytes 2228224 | tf_op jit(solution)/shard_map/while/body/eval_jaxpr/reduce_sum | solution.py:21
  77.1 5.7 %select_reduce_fusion.4 = f32[16,128,256]{2,1,0:T(8,128)S(1)} fusion(f32[16,8,128]{2,1,0:T(8,128)S(1)} %dynamic-slice_bitcast_fusion.4, s32[16,8,128]{2,1,0:T(8,128)S(1)} %dynamic-slice_bitcast_fusion.5), kind=kLoop, calls=%fused_computation.16.clone.1 | loop fusion | flops 12058624 | bytes 2228224 | tf_op jit(solution)/shard_map/while/body/eval_jaxpr/reduce_sum | solution.py:21
  84.2 5.7 %select_reduce_fusion.4 = f32[16,128,256]{2,1,0:T(8,128)S(1)} fusion(f32[16,8,128]{2,1,0:T(8,128)S(1)} %dynamic-slice_bitcast_fusion.4, s32[16,8,128]{2,1,0:T(8,128)S(1)} %dynamic-slice_bitcast_fusion.5), kind=kLoop, calls=%fused_computation.16.clone.1 | loop fusion | flops 12058624 | bytes 2228224 | tf_op jit(solution)/shard_map/while/body/eval_jaxpr/reduce_sum | solution.py:21
  91.5 5.7 %select_reduce_fusion.4 = f32[16,128,256]{2,1,0:T(8,128)S(1)} fusion(f32[16,8,128]{2,1,0:T(8,128)S(1)} %dynamic-slice_bitcast_fusion.4, s32[16,8,128]{2,1,0:T(8,128)S(1)} %dynamic-slice_bitcast_fusion.5), kind=kLoop, calls=%fused_computation.16.clone.1 | loop fusion | flops 12058624 | bytes 2228224 | tf_op jit(solution)/shard_map/while/body/eval_jaxpr/reduce_sum | solution.py:21
  98.7 5.7 %select_reduce_fusion.4 = f32[16,128,256]{2,1,0:T(8,128)S(1)} fusion(f32[16,8,128]{2,1,0:T(8,128)S(1)} %dynamic-slice_bitcast_fusion.4, s32[16,8,128]{2,1,0:T(8,128)S(1)} %dynamic-slice_bitcast_fusion.5), kind=kLoop, calls=%fused_computation.16.clone.1 | loop fusion | flops 12058624 | bytes 2228224 | tf_op jit(solution)/shard_map/while/body/eval_jaxpr/reduce_sum | solution.py:21
  104.4 1.6 bitcast_dynamic-update-slice_fusion.2
  106.0 5.7 %select_reduce_fusion.4 = f32[16,128,256]{2,1,0:T(8,128)S(1)} fusion(f32[16,8,128]{2,1,0:T(8,128)S(1)} %dynamic-slice_bitcast_fusion.4, s32[16,8,128]{2,1,0:T(8,128)S(1)} %dynamic-slice_bitcast_fusion.5), kind=kLoop, calls=%fused_computation.16.clone.1 | loop fusion | flops 12058624 | bytes 2228224 | tf_op jit(solution)/shard_map/while/body/eval_jaxpr/reduce_sum | solution.py:21
  113.1 5.7 %select_reduce_fusion.4 = f32[16,128,256]{2,1,0:T(8,128)S(1)} fusion(f32[16,8,128]{2,1,0:T(8,128)S(1)} %dynamic-slice_bitcast_fusion.4, s32[16,8,128]{2,1,0:T(8,128)S(1)} %dynamic-slice_bitcast_fusion.5), kind=kLoop, calls=%fused_computation.16.clone.1 | loop fusion | flops 12058624 | bytes 2228224 | tf_op jit(solution)/shard_map/while/body/eval_jaxpr/reduce_sum | solution.py:21
  118.8 1.6 bitcast_dynamic-update-slice_fusion.2
  120.4 5.7 %select_reduce_fusion.4 = f32[16,128,256]{2,1,0:T(8,128)S(1)} fusion(f32[16,8,128]{2,1,0:T(8,128)S(1)} %dynamic-slice_bitcast_fusion.4, s32[16,8,128]{2,1,0:T(8,128)S(1)} %dynamic-slice_bitcast_fusion.5), kind=kLoop, calls=%fused_computation.16.clone.1 | loop fusion | flops 12058624 | bytes 2228224 | tf_op jit(solution)/shard_map/while/body/eval_jaxpr/reduce_sum | solution.py:21
  127.6 8.6 %multiply_reduce_fusion.2 = f32[8,16,128]{2,1,0:T(8,128)} fusion(f32[8,16,128,256]{3,2,1,0:T(8,128)} %get-tuple-element.32, f32[8,16,256]{2,1,0:T(8,128)S(1)} %bitcast.63), kind=kLoop, calls=%fused_computation.22 | loop fusion | flops 8372224 | bytes 16973824 | tf_op jit(solution)/shard_map/reduce_sum | solution.py:80
  136.2 41.3 %all-reduce.10.cloned.1.call-done = (f32[128,128]{1,0:T(8,128)}, f32[8,16,128]{2,1,0:T(8,128)}, f32[8,16,128]{2,1,0:T(8,128)}) async-done(((f32[128,128]{1,0:T(8,128)}, f32[8,16,128]{2,1,0:T(8,128)}, f32[8,16,128]{2,1,0:T(8,128)}), (f32[128,128]{1,0:T(8,128)}, f32[8,16,128]{2,1,0:T(8,128)}, f32[8,16,128]{2,1,0:T(8,128)})) %all-reduce.10.cloned.1.call-update) | async-done | bytes 196624 | tf_op jit(solution)/shard_map/psum | solution.py:81
  177.5 10.5 %all_to_all.52 = f32[8,16,128]{2,1,0:T(8,128)S(1)} all-to-all(f32[8,16,128]{2,1,0:T(8,128)} %get-tuple-element.53), channel_id=1, replica_groups=mesh['src'=4,'blk'=8] {'blk'}, dimensions={0} | all-to-all | bytes 131072 | tf_op jit(solution)/shard_map/all_to_all | solution.py:58
  188.0 3.3 %all-to-all-start.4 = ((f32[8,16,128]{2,1,0:T(8,128)}), f32[8,16,128]{2,1,0:T(8,128)S(1)}, u32[]{:S(2)}, u32[]{:S(2)}) async-start(f32[8,16,128]{2,1,0:T(8,128)} %get-tuple-element.52), calls=%async_computation.5 | async-start | bytes 131072 | tf_op jit(solution)/shard_map/all_to_all | solution.py:57
  192.7 4.5 %all-to-all-done.4 = f32[8,16,128]{2,1,0:T(8,128)S(1)} async-done(((f32[8,16,128]{2,1,0:T(8,128)}), f32[8,16,128]{2,1,0:T(8,128)S(1)}, u32[]{:S(2)}, u32[]{:S(2)}) %all-to-all-start.4) | async-done | bytes 65568 | tf_op jit(solution)/shard_map/all_to_all | solution.py:57
  199.5 8.6 %multiply_reduce_fusion.1 = f32[8,16,128]{2,1,0:T(8,128)} fusion(f32[8,16,128,256]{3,2,1,0:T(8,128)} %get-tuple-element.32, f32[8,16,256]{2,1,0:T(8,128)S(1)} %bitcast.65), kind=kLoop, calls=%fused_computation.21 | loop fusion | flops 8372224 | bytes 16973824 | tf_op jit(solution)/shard_map/reduce_sum | solution.py:80
  208.4 39.3 %all-reduce.6.cloned.1.call-done = f32[128,128]{1,0:T(8,128)} async-done(((f32[128,128]{1,0:T(8,128)}), f32[128,128]{1,0:T(8,128)}) %all-reduce.6.cloned.1.call-update) | async-done | bytes 65552 | tf_op jit(solution)/shard_map/psum | solution.py:81
  249.2 8.6 %multiply_reduce_fusion = f32[8,16,128]{2,1,0:T(8,128)} fusion(f32[8,16,128,256]{3,2,1,0:T(8,128)} %get-tuple-element.32, f32[8,16,256]{2,1,0:T(8,128)S(1)} %bitcast.64), kind=kLoop, calls=%fused_computation.20 | loop fusion | flops 8372224 | bytes 16973824 | tf_op jit(solution)/shard_map/reduce_sum | solution.py:80
  257.9 42.0 %all-reduce.8.cloned.1.call-done = f32[128,128]{1,0:T(8,128)} async-done(((f32[128,128]{1,0:T(8,128)}), f32[128,128]{1,0:T(8,128)}) %all-reduce.8.cloned.1.call-update) | async-done | bytes 65552 | tf_op jit(solution)/shard_map/psum | solution.py:81
  302.2 4.6 %all-to-all-start.5 = ((f32[8,16,128]{2,1,0:T(8,128)}), f32[8,16,128]{2,1,0:T(8,128)S(1)}, u32[]{:S(2)}, u32[]{:S(2)}) async-start(f32[8,16,128]{2,1,0:T(8,128)} %broadcast_select_fusion.2), calls=%async_computation.6 | async-start | bytes 131072 | tf_op jit(solution)/shard_map/all_to_all | solution.py:84
  306.8 5.9 %all-to-all-done.5 = f32[8,16,128]{2,1,0:T(8,128)S(1)} async-done(((f32[8,16,128]{2,1,0:T(8,128)}), f32[8,16,128]{2,1,0:T(8,128)S(1)}, u32[]{:S(2)}, u32[]{:S(2)}) %all-to-all-start.5) | async-done | bytes 65568 | tf_op jit(solution)/shard_map/all_to_all | solution.py:84
  (91 shorter events, 30.0 us)
Async XLA Ops:
  6.5 1.9 copy-start
  6.5 21.9 %copy-start.2 = (f32[1,64,128]{2,1,0:T(8,128)S(1)}, f32[1,64,128]{2,1,0:T(8,128)}, u32[]{:S(2)}) copy-start(f32[1,64,128]{2,1,0:T(8,128)} %param.11) | copy-start | bytes 98308
  6.5 21.9 %copy-start.3 = (s32[64,128]{1,0:T(8,128)S(1)}, s32[64,128]{1,0:T(8,128)}, u32[]{:S(2)}) copy-start(s32[64,128]{1,0:T(8,128)} %param.12) | copy-start | bytes 98308
  6.5 22.6 %copy-start.1 = (f32[1,64,128]{2,1,0:T(8,128)S(1)}, f32[1,64,128]{2,1,0:T(8,128)}, u32[]{:S(2)}) copy-start(f32[1,64,128]{2,1,0:T(8,128)} %param.10) | copy-start | bytes 98308
  6.5 42.3 %reduce-scatter.2.cloned.1.call-start = ((), (), s32[]{:S(2)}) async-start(), calls=%async_computation.7 | async-start | bytes 2621440 | tf_op jit(solution)/shard_map/reduce_scatter | solution.py:52
  13.1 11.9 %all-to-all-start = ((s32[8,16,1]{1,2,0:T(1,128)}), s32[8,16,1]{1,2,0:T(1,128)S(1)}, u32[]{:S(2)}, u32[]{:S(2)}) async-start(s32[8,16,1]{1,2,0:T(1,128)} %bitcast.3), calls=%async_computation | async-start | bytes 8192 | tf_op jit(solution)/shard_map/all_to_all | solution.py:62
  24.9 18.8 %all-to-all-start.2 = ((s32[128,8,128]{2,1,0:T(8,128)}), s32[128,8,128]{2,1,0:T(8,128)S(1)}, u32[]{:S(2)}, u32[]{:S(2)}) async-start(s32[128,8,128]{2,1,0:T(8,128)} %constant_dynamic-slice_fusion), calls=%async_computation.2 | async-start | bytes 1048576 | tf_op jit(solution)/shard_map/all_to_all | solution.py:61
  48.9 19.9 %all-to-all-start.3 = ((f32[128,8,128]{2,1,0:T(8,128)}), f32[128,8,128]{2,1,0:T(8,128)S(1)}, u32[]{:S(2)}, u32[]{:S(2)}) async-start(f32[128,8,128]{2,1,0:T(8,128)} %reduce-scatter.2.cloned.1.call-done), calls=%async_computation.4 | async-start | bytes 1048576 | tf_op jit(solution)/shard_map/all_to_all | solution.py:56
  53.5 124.0 %all-reduce.10.cloned.1.call-start = ((), (), s32[]{:S(2)}) async-start(), calls=%async_computation.10 | async-start | bytes 393216 | tf_op jit(solution)/shard_map/psum | solution.py:81
  188.0 9.2 %all-to-all-start.4 = ((f32[8,16,128]{2,1,0:T(8,128)}), f32[8,16,128]{2,1,0:T(8,128)S(1)}, u32[]{:S(2)}, u32[]{:S(2)}) async-start(f32[8,16,128]{2,1,0:T(8,128)} %get-tuple-element.52), calls=%async_computation.5 | async-start | bytes 131072 | tf_op jit(solution)/shard_map/all_to_all | solution.py:57
  191.4 56.3 %all-reduce.6.cloned.1.call-start = ((), (), s32[]{:S(2)}) async-start(), calls=%async_computation.8 | async-start | bytes 131072 | tf_op jit(solution)/shard_map/psum | solution.py:81
  199.5 107.3 %copy-start.4 = (s32[64,1]{0,1:T(1,128)S(1)}, s32[64,1]{0,1:T(1,128)}, u32[]{:S(2)}) copy-start(s32[64,1]{0,1:T(1,128)} %param.14) | copy-start | bytes 772
  208.1 91.7 %all-reduce.8.cloned.1.call-start = ((), (), s32[]{:S(2)}) async-start(), calls=%async_computation.9 | async-start | bytes 131072 | tf_op jit(solution)/shard_map/psum | solution.py:81
  302.2 10.5 %all-to-all-start.5 = ((f32[8,16,128]{2,1,0:T(8,128)}), f32[8,16,128]{2,1,0:T(8,128)S(1)}, u32[]{:S(2)}, u32[]{:S(2)}) async-start(f32[8,16,128]{2,1,0:T(8,128)} %broadcast_select_fusion.2), calls=%async_computation.6 | async-start | bytes 131072 | tf_op jit(solution)/shard_map/all_to_all | solution.py:84
Sparse Core Ops, SparseCore 0:
  10.9 37.9 reduce-scatter.1
  136.4 41.0 all-reduce.9
  208.2 39.3 all-reduce.5
  258.0 41.8 all-reduce.7
where the time goes:
time: 321 us; the launch traced here: 320 us
  waiting for transfers between devices  163 us (51%)
  other arithmetic  82.2 us (26%)
  local copies, waits for them, and re-layouts  27 us (8%)
  starting transfers between devices  22.7 us (7%)
  between operations  14.7 us (5%)
  blocking collectives  10.5 us (3%)
    psum x3, waiting for transfers between devices, on_device(): summed = lax.psum(partial_sum, 'src')  123 us
    reduce_sum x8, other arithmetic, build(): return jnp.sum(picked, axis=1)  45.3 us
    reduce_sum x3, other arithmetic, on_device(): partial_sum = jnp.sum(dense * nearby[:, None, :], axis=2)  25.9 us
    all_to_all x1, waiting for transfers between devices, on_device(): lax.all_to_all(part_vals, 'blk', split_axis=0, concat_axis=0, tiled=True)  13.3 us
    dynamic_update_slice x8, local copies, waits for them, and re-layouts, tile_matrix(): dense = lax.map(build, (grouped_vals, grouped_lanes))  12.3 us
    all_to_all x1, blocking collectives, on_device(): lax.all_to_all(sum_rhs, 'blk', split_axis=0, concat_axis=0, tiled=True)  10.5 us
    all_to_all x1, waiting for transfers between devices, on_device(): lax.all_to_all(part_cols, 'blk', split_axis=0, concat_axis=0, tiled=True)  9.16 us
  transfers between devices with their start and end apart: 9, of which 9 were waited for; matrix products, arithmetic and copies ran while one was open for 4% of the time, Pallas kernels for 0%

commit v1 on v0

--- a/solution.py
+++ b/solution.py
@@ -4,6 +4,11 @@
 from jax.sharding import PartitionSpec as P
 
 SWEEPS = 3
+
+
+def summed_here(array, axis):
+    shards = lax.all_gather(array, axis)
+    return jnp.sum(shards, axis=0)
 
 
 def tile_matrix(block_vals, block_cols, tile_rows):
@@ -78,7 +83,7 @@
     for sweep_index in range(SWEEPS):
         nearby = jnp.concatenate([iterate, iterate[following]], axis=1)
         partial_sum = jnp.sum(dense * nearby[:, None, :], axis=2)
-        summed = lax.psum(partial_sum, "src")
+        summed = summed_here(partial_sum, "src")
         iterate = jnp.where(occupied[:, None], (right_side - summed) / block_diag, 0.0)
     in_slots = jnp.where(is_live[:, None], iterate[tile_rank], 0.0)
     returned = lax.all_to_all(in_slots, "blk", split_axis=0, concat_axis=0, tiled=True)

time: 321 us -> 246 us (0.77)
  waiting for transfers between devices: 163 us -> 67 us
  blocking collectives: 10.5 us -> 38 us
  starting transfers between devices: 22.7 us -> 19.1 us
  other arithmetic: 82.2 us -> 78.7 us
    psum x3 -> x1, waiting for transfers between devices: 123 us -> 29.3 us  [on_device(): sum_diag, sum_rhs = lax.psum((send_diag, send_rhs), 'src')]
    all_gather x0 -> x3, blocking collectives: none -> 26.3 us  [summed_here(): shards = lax.all_gather(array, axis)]
    reduce_scatter x1, waiting for transfers between devices: 5.18 us -> 0.01 us  [on_device(): lax.psum_scatter(send_vals, 'src', scatter_dimension=1, tiled=True)]
  transfers between devices with their start and end apart: 9 -> 7, of which waited for: 9 -> 6; matrix products, arithmetic and copies ran while one was open for 4% -> 5% of each run, Pallas kernels for 0% -> 0%
where the time goes in v1:
time: 246 us; the launch traced here: 245 us
  other arithmetic  78.7 us (32%)
  waiting for transfers between devices  67 us (27%)
  blocking collectives  38 us (15%)
  local copies, waits for them, and re-layouts  26.9 us (11%)
  starting transfers between devices  19.1 us (8%)
  between operations  15 us (6%)
    reduce_sum x8, other arithmetic, build(): return jnp.sum(picked, axis=1)  45.3 us
    psum x1, waiting for transfers between devices, on_device(): sum_diag, sum_rhs = lax.psum((send_diag, send_rhs), 'src')  29.3 us
    all_gather x3, blocking collectives, summed_here(): shards = lax.all_gather(array, axis)  26.3 us
    reduce_sum x3, other arithmetic, on_device(): partial_sum = jnp.sum(dense * nearby[:, None, :], axis=2)  24 us
    all_to_all x1, waiting for transfers between devices, on_device(): lax.all_to_all(part_vals, 'blk', split_axis=0, concat_axis=0, tiled=True)  13 us
    dynamic_update_slice x8, local copies, waits for them, and re-layouts, tile_matrix(): dense = lax.map(build, (grouped_vals, grouped_lanes))  12.3 us
    all_to_all x1, blocking collectives, on_device(): lax.all_to_all(send_keys, 'blk', split_axis=0, concat_axis=0, tiled=True)  11.7 us
    all_to_all x1, waiting for transfers between devices, on_device(): lax.all_to_all(part_cols, 'blk', split_axis=0, concat_axis=0, tiled=True)  9.86 us
  transfers between devices with their start and end apart: 7, of which 6 were waited for; matrix products, arithmetic and copies ran while one was open for 5% of the time, Pallas kernels for 0%

profile of v1, /device:TPU:0, one launch (start us, length us, event | category | flops | bytes accessed | tf_op | source)
XLA Modules:
  0.0 244.8 jit_solution(5694291346666444372)
XLA Ops:
  12.8 1.6 broadcast_select_fusion
  14.4 1.6 gather_fusion
  16.1 11.7 %all_to_all.52 = s32[8,16,1]{1,2,0:T(1,128)S(1)} all-to-all(s32[8,16,1]{1,2,0:T(1,128)S(1)} %bitcast.83), channel_id=1, replica_groups=mesh['src'=4,'blk'=8] {'blk'}, dimensions={0} | all-to-all | bytes 1024 | tf_op jit(solution)/shard_map/all_to_all | solution.py:67
  27.8 29.3 %all-reduce.4.cloned.1.call-done = (f32[8,16,128]{2,1,0:T(8,128)}, f32[8,16,128]{2,1,0:T(8,128)}) async-done(((f32[8,16,128]{2,1,0:T(8,128)}, f32[8,16,128]{2,1,0:T(8,128)}), (f32[8,16,128]{2,1,0:T(8,128)}, f32[8,16,128]{2,1,0:T(8,128)})) %all-reduce.4.cloned.1.call-update) | async-done | bytes 131088 | tf_op jit(solution)/shard_map/psum | solution.py:58
  57.1 4.6 %all-to-all-start.1 = ((f32[8,16,128]{2,1,0:T(8,128)}), f32[8,16,128]{2,1,0:T(8,128)S(1)}, u32[]{:S(2)}, u32[]{:S(2)}) async-start(f32[8,16,128]{2,1,0:T(8,128)} %get-tuple-element.52), calls=%async_computation.1 | async-start | bytes 131072 | tf_op jit(solution)/shard_map/all_to_all | solution.py:63
  61.7 1.9 gather_fusion.3
  63.6 4.0 %all-to-all-done.1 = f32[8,16,128]{2,1,0:T(8,128)S(1)} async-done(((f32[8,16,128]{2,1,0:T(8,128)}), f32[8,16,128]{2,1,0:T(8,128)S(1)}, u32[]{:S(2)}, u32[]{:S(2)}) %all-to-all-start.1) | async-done | bytes 65568 | tf_op jit(solution)/shard_map/all_to_all | solution.py:63
  67.6 3.3 %all-to-all-start.4 = ((f32[8,16,128]{2,1,0:T(8,128)}), f32[8,16,128]{2,1,0:T(8,128)S(1)}, u32[]{:S(2)}, u32[]{:S(2)}) async-start(f32[8,16,128]{2,1,0:T(8,128)} %get-tuple-element.51), calls=%async_computation.5 | async-start | bytes 131072 | tf_op jit(solution)/shard_map/all_to_all | solution.py:62
  71.9 5.0 %all-to-all-done.4 = f32[8,16,128]{2,1,0:T(8,128)S(1)} async-done(((f32[8,16,128]{2,1,0:T(8,128)}), f32[8,16,128]{2,1,0:T(8,128)S(1)}, u32[]{:S(2)}, u32[]{:S(2)}) %all-to-all-start.4) | async-done | bytes 65568 | tf_op jit(solution)/shard_map/all_to_all | solution.py:62
  76.8 3.5 %all-to-all-start.2 = ((s32[128,8,128]{2,1,0:T(8,128)}), s32[128,8,128]{2,1,0:T(8,128)S(1)}, u32[]{:S(2)}, u32[]{:S(2)}) async-start(s32[128,8,128]{2,1,0:T(8,128)} %constant_dynamic-slice_fusion), calls=%async_computation.2 | async-start | bytes 1048576 | tf_op jit(solution)/shard_map/all_to_all | solution.py:66
  85.7 9.9 %all-to-all-done.2 = s32[128,8,128]{2,1,0:T(8,128)S(1)} async-done(((s32[128,8,128]{2,1,0:T(8,128)}), s32[128,8,128]{2,1,0:T(8,128)S(1)}, u32[]{:S(2)}, u32[]{:S(2)}) %all-to-all-start.2) | async-done | bytes 524320 | tf_op jit(solution)/shard_map/all_to_all | solution.py:66
  95.6 4.3 %all-to-all-start.3 = ((f32[128,8,128]{2,1,0:T(8,128)}), f32[128,8,128]{2,1,0:T(8,128)S(1)}, u32[]{:S(2)}, u32[]{:S(2)}) async-start(f32[128,8,128]{2,1,0:T(8,128)} %reduce-scatter.2.cloned.1.call-done), calls=%async_computation.4 | async-start | bytes 1048576 | tf_op jit(solution)/shard_map/all_to_all | solution.py:61
  102.2 13.0 %all-to-all-done.3 = f32[128,8,128]{2,1,0:T(8,128)S(1)} async-done(((f32[128,8,128]{2,1,0:T(8,128)}), f32[128,8,128]{2,1,0:T(8,128)S(1)}, u32[]{:S(2)}, u32[]{:S(2)}) %all-to-all-start.3) | async-done | bytes 524320 | tf_op jit(solution)/shard_map/all_to_all | solution.py:61
  116.2 57.8 %while.11 = (s32[]{:T(128)}, f32[8,16,128,256]{3,2,1,0:T(8,128)}, s32[8,16,8,128]{3,2,1,0:T(8,128)S(1)}, f32[8,16,8,128]{3,2,1,0:T(8,128)S(1)}, s32[]{:T(128)}) while((s32[]{:T(128)}, f32[8,16,128,256]{3,2,1,0:T(8,128)}, s32[8,16,8,128]{3,2,1,0:T(8,128)S(1)}, f32[8,16,8,128]{3,2,1,0:T(8,128)S(1)}, s32[]{:T(128)}) %tuple.23), condition=%wide.region_10.11_spmd.clone, body=%wide.region_8.10_spmd.clone.sunk | while | flops 12058626 | bytes 6685253 | solution.py:28
  116.2 5.7 %select_reduce_fusion.4 = f32[16,128,256]{2,1,0:T(8,128)S(1)} fusion(f32[16,8,128]{2,1,0:T(8,128)S(1)} %dynamic-slice_bitcast_fusion.4, s32[16,8,128]{2,1,0:T(8,128)S(1)} %dynamic-slice_bitcast_fusion.5), kind=kLoop, calls=%fused_computation.16.clone.1 | loop fusion | flops 12058624 | bytes 2228224 | tf_op jit(solution)/shard_map/while/body/eval_jaxpr/reduce_sum | solution.py:26
  123.5 5.7 %select_reduce_fusion.4 = f32[16,128,256]{2,1,0:T(8,128)S(1)} fusion(f32[16,8,128]{2,1,0:T(8,128)S(1)} %dynamic-slice_bitcast_fusion.4, s32[16,8,128]{2,1,0:T(8,128)S(1)} %dynamic-slice_bitcast_fusion.5), kind=kLoop, calls=%fused_computation.16.clone.1 | loop fusion | flops 12058624 | bytes 2228224 | tf_op jit(solution)/shard_map/while/body/eval_jaxpr/reduce_sum | solution.py:26
  130.6 5.7 %select_reduce_fusion.4 = f32[16,128,256]{2,1,0:T(8,128)S(1)} fusion(f32[16,8,128]{2,1,0:T(8,128)S(1)} %dynamic-slice_bitcast_fusion.4, s32[16,8,128]{2,1,0:T(8,128)S(1)} %dynamic-slice_bitcast_fusion.5), kind=kLoop, calls=%fused_computation.16.clone.1 | loop fusion | flops 12058624 | bytes 2228224 | tf_op jit(solution)/shard_map/while/body/eval_jaxpr/reduce_sum | solution.py:26
  137.9 5.7 %select_reduce_fusion.4 = f32[16,128,256]{2,1,0:T(8,128)S(1)} fusion(f32[16,8,128]{2,1,0:T(8,128)S(1)} %dynamic-slice_bitcast_fusion.4, s32[16,8,128]{2,1,0:T(8,128)S(1)} %dynamic-slice_bitcast_fusion.5), kind=kLoop, calls=%fused_computation.16.clone.1 | loop fusion | flops 12058624 | bytes 2228224 | tf_op jit(solution)/shard_map/while/body/eval_jaxpr/reduce_sum | solution.py:26
  145.1 5.7 %select_reduce_fusion.4 = f32[16,128,256]{2,1,0:T(8,128)S(1)} fusion(f32[16,8,128]{2,1,0:T(8,128)S(1)} %dynamic-slice_bitcast_fusion.4, s32[16,8,128]{2,1,0:T(8,128)S(1)} %dynamic-slice_bitcast_fusion.5), kind=kLoop, calls=%fused_computation.16.clone.1 | loop fusion | flops 12058624 | bytes 2228224 | tf_op jit(solution)/shard_map/while/body/eval_jaxpr/reduce_sum | solution.py:26
  150.8 1.6 bitcast_dynamic-update-slice_fusion.2
  152.4 5.7 %select_reduce_fusion.4 = f32[16,128,256]{2,1,0:T(8,128)S(1)} fusion(f32[16,8,128]{2,1,0:T(8,128)S(1)} %dynamic-slice_bitcast_fusion.4, s32[16,8,128]{2,1,0:T(8,128)S(1)} %dynamic-slice_bitcast_fusion.5), kind=kLoop, calls=%fused_computation.16.clone.1 | loop fusion | flops 12058624 | bytes 2228224 | tf_op jit(solution)/shard_map/while/body/eval_jaxpr/reduce_sum | solution.py:26
  159.5 5.7 %select_reduce_fusion.4 = f32[16,128,256]{2,1,0:T(8,128)S(1)} fusion(f32[16,8,128]{2,1,0:T(8,128)S(1)} %dynamic-slice_bitcast_fusion.4, s32[16,8,128]{2,1,0:T(8,128)S(1)} %dynamic-slice_bitcast_fusion.5), kind=kLoop, calls=%fused_computation.16.clone.1 | loop fusion | flops 12058624 | bytes 2228224 | tf_op jit(solution)/shard_map/while/body/eval_jaxpr/reduce_sum | solution.py:26
  165.2 1.6 bitcast_dynamic-update-slice_fusion.2
  166.8 5.7 %select_reduce_fusion.4 = f32[16,128,256]{2,1,0:T(8,128)S(1)} fusion(f32[16,8,128]{2,1,0:T(8,128)S(1)} %dynamic-slice_bitcast_fusion.4, s32[16,8,128]{2,1,0:T(8,128)S(1)} %dynamic-slice_bitcast_fusion.5), kind=kLoop, calls=%fused_computation.16.clone.1 | loop fusion | flops 12058624 | bytes 2228224 | tf_op jit(solution)/shard_map/while/body/eval_jaxpr/reduce_sum | solution.py:26
  174.0 8.0 %multiply_reduce_fusion.2 = f32[8,16,128]{2,1,0:T(8,128)S(1)} fusion(f32[8,16,128,256]{3,2,1,0:T(8,128)} %get-tuple-element.32, f32[8,16,256]{2,1,0:T(8,128)S(1)} %bitcast.73), kind=kLoop, calls=%fused_computation.22 | loop fusion | flops 8372224 | bytes 16973824 | tf_op jit(solution)/shard_map/reduce_sum | solution.py:85
  182.0 9.1 %all_gather.19 = f32[4,128,128]{2,1,0:T(8,128)S(1)} all-gather(f32[1,128,128]{2,1,0:T(8,128)S(1)} %bitcast.75), channel_id=1, replica_groups=mesh['src'=4,'blk'=8] {'src'}, dimensions={0}, use_global_device_ids=true | all-gather | bytes 327680 | tf_op jit(solution)/shard_map/all_gather | solution.py:10
  192.0 8.0 %multiply_reduce_fusion.1 = f32[8,16,128]{2,1,0:T(8,128)S(1)} fusion(f32[8,16,128,256]{3,2,1,0:T(8,128)} %get-tuple-element.32, f32[8,16,256]{2,1,0:T(8,128)S(1)} %pad_maximum_fusion), kind=kLoop, calls=%fused_computation.21 | loop fusion | flops 8372224 | bytes 16973824 | tf_op jit(solution)/shard_map/reduce_sum | solution.py:85
  200.0 8.1 %all_gather.21 = f32[4,128,128]{2,1,0:T(8,128)S(1)} all-gather(f32[1,128,128]{2,1,0:T(8,128)S(1)} %bitcast.76), channel_id=1, replica_groups=mesh['src'=4,'blk'=8] {'src'}, dimensions={0}, use_global_device_ids=true | all-gather | bytes 327680 | tf_op jit(solution)/shard_map/all_gather | solution.py:10
  209.0 8.0 %multiply_reduce_fusion = f32[8,16,128]{2,1,0:T(8,128)S(1)} fusion(f32[8,16,128,256]{3,2,1,0:T(8,128)} %get-tuple-element.32, f32[8,16,256]{2,1,0:T(8,128)S(1)} %pad_maximum_fusion.1), kind=kLoop, calls=%fused_computation.20 | loop fusion | flops 8372224 | bytes 16973824 | tf_op jit(solution)/shard_map/reduce_sum | solution.py:85
  217.0 9.1 %all_gather.23 = f32[4,128,128]{2,1,0:T(8,128)S(1)} all-gather(f32[1,128,128]{2,1,0:T(8,128)S(1)} %bitcast.74), channel_id=1, replica_groups=mesh['src'=4,'blk'=8] {'src'}, dimensions={0}, use_global_device_ids=true | all-gather | bytes 327680 | tf_op jit(solution)/shard_map/all_gather | solution.py:10
  227.5 3.3 %all-to-all-start.5 = ((f32[8,16,128]{2,1,0:T(8,128)}), f32[8,16,128]{2,1,0:T(8,128)S(1)}, u32[]{:S(2)}, u32[]{:S(2)}) async-start(f32[8,16,128]{2,1,0:T(8,128)} %broadcast_select_fusion.2), calls=%async_computation.6 | async-start | bytes 131072 | tf_op jit(solution)/shard_map/all_to_all | solution.py:89
  230.9 5.8 %all-to-all-done.5 = f32[8,16,128]{2,1,0:T(8,128)S(1)} async-done(((f32[8,16,128]{2,1,0:T(8,128)}), f32[8,16,128]{2,1,0:T(8,128)S(1)}, u32[]{:S(2)}, u32[]{:S(2)}) %all-to-all-start.5) | async-done | bytes 65568 | tf_op jit(solution)/shard_map/all_to_all | solution.py:89
  (87 shorter events, 28.2 us)
Async XLA Ops:
  6.5 5.5 %copy-start = (f32[1,64,32,128]{3,2,1,0:T(8,128)S(1)}, f32[1,64,32,128]{3,2,1,0:T(8,128)}, u32[]{:S(2)}) copy-start(f32[1,64,32,128]{3,2,1,0:T(8,128)} %param.9) | copy-start | bytes 3145732
  6.5 50.6 %all-reduce.4.cloned.1.call-start = ((), (), s32[]{:S(2)}) async-start(), calls=%async_computation.8 | async-start | bytes 262144 | tf_op jit(solution)/shard_map/psum | solution.py:58
  11.9 83.6 %reduce-scatter.2.cloned.1.call-start = ((), (), s32[]{:S(2)}) async-start(), calls=%async_computation.7 | async-start | bytes 2621440 | tf_op jit(solution)/shard_map/reduce_scatter | solution.py:57
  57.1 10.5 %all-to-all-start.1 = ((f32[8,16,128]{2,1,0:T(8,128)}), f32[8,16,128]{2,1,0:T(8,128)S(1)}, u32[]{:S(2)}, u32[]{:S(2)}) async-start(f32[8,16,128]{2,1,0:T(8,128)} %get-tuple-element.52), calls=%async_computation.1 | async-start | bytes 131072 | tf_op jit(solution)/shard_map/all_to_all | solution.py:63
  67.6 9.2 %all-to-all-start.4 = ((f32[8,16,128]{2,1,0:T(8,128)}), f32[8,16,128]{2,1,0:T(8,128)S(1)}, u32[]{:S(2)}, u32[]{:S(2)}) async-start(f32[8,16,128]{2,1,0:T(8,128)} %get-tuple-element.51), calls=%async_computation.5 | async-start | bytes 131072 | tf_op jit(solution)/shard_map/all_to_all | solution.py:62
  76.8 18.8 %all-to-all-start.2 = ((s32[128,8,128]{2,1,0:T(8,128)}), s32[128,8,128]{2,1,0:T(8,128)S(1)}, u32[]{:S(2)}, u32[]{:S(2)}) async-start(s32[128,8,128]{2,1,0:T(8,128)} %constant_dynamic-slice_fusion), calls=%async_computation.2 | async-start | bytes 1048576 | tf_op jit(solution)/shard_map/all_to_all | solution.py:66
  95.6 19.6 %all-to-all-start.3 = ((f32[128,8,128]{2,1,0:T(8,128)}), f32[128,8,128]{2,1,0:T(8,128)S(1)}, u32[]{:S(2)}, u32[]{:S(2)}) async-start(f32[128,8,128]{2,1,0:T(8,128)} %reduce-scatter.2.cloned.1.call-done), calls=%async_computation.4 | async-start | bytes 1048576 | tf_op jit(solution)/shard_map/all_to_all | solution.py:61
  192.0 38.9 %copy-start.1 = (s32[64,1]{0,1:T(1,128)S(1)}, s32[64,1]{0,1:T(1,128)}, u32[]{:S(2)}) copy-start(s32[64,1]{0,1:T(1,128)} %param.14) | copy-start | bytes 772
  227.5 9.2 %all-to-all-start.5 = ((f32[8,16,128]{2,1,0:T(8,128)}), f32[8,16,128]{2,1,0:T(8,128)S(1)}, u32[]{:S(2)}, u32[]{:S(2)}) async-start(f32[8,16,128]{2,1,0:T(8,128)} %broadcast_select_fusion.2), calls=%async_computation.6 | async-start | bytes 131072 | tf_op jit(solution)/shard_map/all_to_all | solution.py:89
Sparse Core Ops, SparseCore 0:
  12.1 44.9 all-reduce.3
  60.1 35.1 reduce-scatter.1
